TPU v7x, 32 devices: a whole 2x2x4 slice. The times are simulated.
32 devices in a mesh: dp: 8 (over y, x, core), seq: 4 (over z).
Axes of the slice: x: 2, y: 2, z: 4, core: 2. Of those that a mesh axis runs over, the one named last changes fastest.
Arguments:
- block_input: bfloat16 [16, 512, 2048], P('dp', 'seq'), may hold values from -12 to 12
- segment_ids: int32 [16, 512], P('dp'), may hold values from 0 to 3, never falling along the last dimension, each value on 1 to 256 neighbouring positions
- cotangent: bfloat16 [16, 512, 2048], P('dp', 'seq'), may hold values from -6 to 6
- attn_gain: float32 [2048], P(('dp', 'seq')), may hold values from 0.5 to 1.5
- qkv_weight: float32 [2048, 3072], P('dp', 'seq'), may hold values from -1 to 1
- out_weight: float32 [2048, 2048], P('seq', 'dp'), may hold values from -0.75 to 0.75
- mlp_gain: float32 [2048], P(('dp', 'seq')), may hold values from 0.5 to 1.5
- gate_up_weight: float32 [2048, 2, 8192], P('dp', None, 'seq'), may hold values from -0.125 to 0.125
- down_weight: float32 [8192, 2048], P('seq', 'dp'), may hold values from -0.125 to 0.125
- first_attn_gain: float32 [2048], P(('dp', 'seq')), may hold values from -30 to 30
- first_qkv: float32 [2048, 3072], P('dp', 'seq'), may hold values from -30 to 30
- first_out: float32 [2048, 2048], P('seq', 'dp'), may hold values from -30 to 30
- first_mlp_gain: float32 [2048], P(('dp', 'seq')), may hold values from -30 to 30
- first_gate_up: float32 [2048, 2, 8192], P('dp', None, 'seq'), may hold values from -30 to 30
- first_down: float32 [8192, 2048], P('seq', 'dp'), may hold values from -30 to 30
- second_attn_gain: float32 [2048], P(('dp', 'seq')), may hold values from 100 to 300000
- second_qkv: float32 [2048, 3072], P('dp', 'seq'), may hold values from 100 to 30000
- second_out: float32 [2048, 2048], P('seq', 'dp'), may hold values from 50 to 500
- second_mlp_gain: float32 [2048], P(('dp', 'seq')), may hold values from 50 to 500
- second_gate_up: float32 [2048, 2, 8192], P('dp', None, 'seq'), may hold values from 50 to 500
- second_down: float32 [8192, 2048], P('seq', 'dp'), may hold values from 50 to 500
Outputs:
- output: bfloat16 [16, 512, 2048], P('dp', 'seq')
- input_grad: bfloat16 [16, 512, 2048], P('dp', 'seq')
- grad_attn_gain: float32 [2048], P(('dp', 'seq'))
- grad_qkv: float32 [2048, 3072], P('dp', 'seq')
- grad_out: float32 [2048, 2048], P('seq', 'dp')
- grad_mlp_gain: float32 [2048], P(('dp', 'seq'))
- grad_gate_up: float32 [2048, 2, 8192], P('dp', None, 'seq')
- grad_down: float32 [8192, 2048], P('seq', 'dp')
- new_attn_gain: float32 [2048], P(('dp', 'seq'))
- new_qkv: float32 [2048, 3072], P('dp', 'seq')
- new_out: float32 [2048, 2048], P('seq', 'dp')
- new_mlp_gain: float32 [2048], P(('dp', 'seq'))
- new_gate_up: float32 [2048, 2, 8192], P('dp', None, 'seq')
- new_down: float32 [8192, 2048], P('seq', 'dp')
- new_first_attn_gain: float32 [2048], P(('dp', 'seq'))
- new_first_qkv: float32 [2048, 3072], P('dp', 'seq')
- new_first_out: float32 [2048, 2048], P('seq', 'dp')
- new_first_mlp_gain: float32 [2048], P(('dp', 'seq'))
- new_first_gate_up: float32 [2048, 2, 8192], P('dp', None, 'seq')
- new_first_down: float32 [8192, 2048], P('seq', 'dp')
- new_second_attn_gain: float32 [2048], P(('dp', 'seq'))
- new_second_qkv: float32 [2048, 3072], P('dp', 'seq')
- new_second_out: float32 [2048, 2048], P('seq', 'dp')
- new_second_mlp_gain: float32 [2048], P(('dp', 'seq'))
- new_second_gate_up: float32 [2048, 2, 8192], P('dp', None, 'seq')
- new_second_down: float32 [8192, 2048], P('seq', 'dp')
Inputs may be any that keep to these rules, and one draw needn't show every extreme that they name: `segment_ids`: in each sequence the numbers never fall, and each segment holds 1 to 256 consecutive positions, one of them exactly that many.
All inputs are finite; a program needn't handle non-finite values.
Results may differ from a plain program's by a relative error of at most 0.023.
Values may be sent and summed in bfloat16 or wider, within the bound.
A program may use at most 320 MiB of HBM per device.

v0:
```python
import jax
import jax.numpy as jnp
from jax import lax
from jax.sharding import PartitionSpec as P

HEADS = 32
KV_HEADS = 8
HEAD_DIM = 64
norm_eps = 1e-05
rope_base = 500000.0
beta_one = 0.9
beta_two = 0.95
learn_rate = 0.01
weight_decay = 0.1
adam_eps = 1e-08
step_count = 10.0
masked_score = -1e30


def segment_positions(segments):
    length_here = segments.shape[-1]
    earlier = (segments[..., None, :] < segments[..., :, None]).astype(jnp.int32)
    return jnp.arange(length_here, dtype=jnp.int32) - jnp.sum(earlier, axis=-1, dtype=jnp.int32)


def rope_tables(positions, head_size):
    half_size = head_size // 2
    inverse = rope_base ** (-2.0 * jnp.arange(half_size, dtype=jnp.float32) / head_size)
    angles = positions.astype(jnp.float32)[..., None] * inverse
    return (jnp.cos(angles), jnp.sin(angles))


def rotate(vectors, cosine, sine):
    half_size = vectors.shape[-1] // 2
    first_half = vectors[..., :half_size]
    second_half = vectors[..., half_size:]
    cos_wide = cosine[..., None, :]
    sin_wide = sine[..., None, :]
    return jnp.concatenate(
        [
            first_half * cos_wide - second_half * sin_wide,
            second_half * cos_wide + first_half * sin_wide,
        ],
        -1,
    )


def unrotate(vectors, cosine, sine):
    half_size = vectors.shape[-1] // 2
    first_half = vectors[..., :half_size]
    second_half = vectors[..., half_size:]
    cos_wide = cosine[..., None, :]
    sin_wide = sine[..., None, :]
    return jnp.concatenate(
        [
            first_half * cos_wide + second_half * sin_wide,
            second_half * cos_wide - first_half * sin_wide,
        ],
        -1,
    )


def rms_forward(values, gain_wide):
    inverse = lax.rsqrt(jnp.mean(values * values, axis=-1, keepdims=True) + norm_eps)
    scaled = values * inverse
    return (scaled, inverse, (scaled * gain_wide).astype(jnp.bfloat16))


def rms_backward(d_normed, scaled, inverse, gain_wide):
    d_scaled = d_normed * gain_wide
    d_values = inverse * (d_scaled - scaled * jnp.mean(d_scaled * scaled, axis=-1, keepdims=True))
    return (d_values, jnp.sum(d_normed * scaled, axis=0))


def adam_update(weight, grad, first, second):
    new_first = beta_one * first + (1.0 - beta_one) * grad
    new_second = beta_two * second + (1.0 - beta_two) * grad * grad
    first_hat = new_first / (1.0 - beta_one**step_count)
    second_hat = new_second / (1.0 - beta_two**step_count)
    new_weight = weight - learn_rate * (
        first_hat / (jnp.sqrt(second_hat) + adam_eps) + weight_decay * weight
    )
    return (new_weight, new_first, new_second)


def contract_rows(left, right):
    return lax.dot_general(
        left, right, (((0,), (0,)), ((), ())), preferred_element_type=jnp.float32
    )


def times_transpose(left, right):
    return lax.dot_general(
        left, right, (((1,), (1,)), ((), ())), preferred_element_type=jnp.float32
    )


def per_device(
    block_input,
    segment_ids,
    cotangent,
    attn_gain,
    qkv_weight,
    out_weight,
    mlp_gain,
    gate_up_weight,
    down_weight,
    first_attn_gain,
    first_qkv,
    first_out,
    first_mlp_gain,
    first_gate_up,
    first_down,
    second_attn_gain,
    second_qkv,
    second_out,
    second_mlp_gain,
    second_gate_up,
    second_down,
):
    seqs_here, local_len, width = block_input.shape
    full_len = segment_ids.shape[1]
    total_rows = seqs_here * full_len
    groups = HEADS // KV_HEADS
    slot_count = groups + 2
    kv_local = qkv_weight.shape[1] // (slot_count * HEAD_DIM)
    query_cols = kv_local * groups * HEAD_DIM
    unit_count = down_weight.shape[0]
    score_scale = HEAD_DIM ** (-0.5)
    local_rows = seqs_here * local_len
    gain_pair = jnp.stack([attn_gain, mlp_gain]).astype(jnp.bfloat16)
    gain_block = lax.all_gather(gain_pair, ("dp", "seq"), axis=1, tiled=True)
    gain_one = gain_block[0].astype(jnp.float32)
    gain_two = gain_block[1].astype(jnp.float32)
    local_input = block_input.reshape(local_rows, width).astype(jnp.float32)
    scaled_one, inverse_one, normed_here = rms_forward(local_input, gain_one)
    normed_one = lax.all_gather(
        normed_here.reshape(seqs_here, local_len, width), "seq", axis=1, tiled=True
    ).reshape(total_rows, width)
    qkv_cols = lax.all_gather(qkv_weight.astype(jnp.bfloat16), "dp", axis=0, tiled=True)
    out_rows = lax.all_gather(out_weight.astype(jnp.bfloat16), "dp", axis=1, tiled=True)
    gate_up_cols = lax.all_gather(
        gate_up_weight.astype(jnp.bfloat16).reshape(-1, 2 * unit_count), "dp", axis=0, tiled=True
    )
    cot_all = lax.all_gather(cotangent, "seq", axis=1, tiled=True)
    down_rows = lax.all_gather(down_weight.astype(jnp.bfloat16), "dp", axis=1, tiled=True)
    positions = segment_positions(segment_ids)
    cosine, sine = rope_tables(positions, HEAD_DIM)
    index_line = jnp.arange(full_len, dtype=jnp.int32)
    allowed = (segment_ids[:, :, None] == segment_ids[:, None, :]) & (
        index_line[None, None, :] <= index_line[None, :, None]
    )
    allowed = allowed[:, None, None, :, :]
    qkv = jnp.dot(normed_one, qkv_cols, preferred_element_type=jnp.float32)
    qkv = qkv.reshape(seqs_here, full_len, kv_local, slot_count, HEAD_DIM)
    query = qkv[:, :, :, :groups].reshape(seqs_here, full_len, kv_local * groups, HEAD_DIM)
    query_groups = (
        rotate(query, cosine, sine)
        .astype(jnp.bfloat16)
        .reshape(seqs_here, full_len, kv_local, groups, HEAD_DIM)
    )
    key16 = rotate(qkv[:, :, :, groups], cosine, sine).astype(jnp.bfloat16)
    value16 = qkv[:, :, :, groups + 1].astype(jnp.bfloat16)

    def masked_scores():
        raw_scores = (
            jnp.einsum("sqgjd,skgd->sgjqk", query_groups, key16, preferred_element_type=jnp.float32)
            * score_scale
        )
        return jnp.where(allowed, raw_scores, masked_score)

    scores = masked_scores()
    top_score = jnp.max(scores, axis=-1, keepdims=True)
    log_total = top_score + jnp.log(jnp.sum(jnp.exp(scores - top_score), axis=-1, keepdims=True))
    probs16 = jnp.exp(scores - log_total).astype(jnp.bfloat16)
    attended16 = jnp.einsum(
        "sgjqk,skgd->sqgjd", probs16, value16, preferred_element_type=jnp.float32
    )
    attended16 = attended16.reshape(total_rows, query_cols).astype(jnp.bfloat16)
    attn_part = jnp.dot(attended16, out_rows, preferred_element_type=jnp.float32)

    def to_local(part):
        return (
            lax.psum_scatter(
                part.astype(jnp.bfloat16).reshape(seqs_here, full_len, width),
                "seq",
                scatter_dimension=1,
                tiled=True,
            )
            .astype(jnp.float32)
            .reshape(local_rows, width)
        )

    resid = local_input + to_local(attn_part)
    scaled_two, inverse_two, normed_two_here = rms_forward(resid, gain_two)
    normed_two = lax.all_gather(
        normed_two_here.reshape(seqs_here, local_len, width), "seq", axis=1, tiled=True
    ).reshape(total_rows, width)
    gate_up = jnp.dot(normed_two, gate_up_cols, preferred_element_type=jnp.float32)
    gate_part = gate_up[:, :unit_count]
    up_part = gate_up[:, unit_count:]
    sigmoid_gate = jax.nn.sigmoid(gate_part)
    active = gate_part * sigmoid_gate
    hidden16 = (active * up_part).astype(jnp.bfloat16)
    down_part = jnp.dot(hidden16, down_rows, preferred_element_type=jnp.float32)
    output = (resid + to_local(down_part)).astype(jnp.bfloat16).reshape(block_input.shape)
    cot_rows = cot_all.reshape(total_rows, width)
    d_hidden = times_transpose(cot_rows, down_rows)
    d_gate = d_hidden * up_part * sigmoid_gate * (1.0 + gate_part * (1.0 - sigmoid_gate))
    d_up = d_hidden * active
    d_gate_up16 = jnp.concatenate([d_gate, d_up], 1).astype(jnp.bfloat16)
    d_normed_two = to_local(times_transpose(d_gate_up16, gate_up_cols))
    down_term = contract_rows(cot_rows, hidden16)
    gate_up_term = contract_rows(normed_two, d_gate_up16)
    down_sum = lax.psum_scatter(
        down_term.astype(jnp.bfloat16), "dp", scatter_dimension=0, tiled=True
    ).astype(jnp.float32)
    grad_gate_up = (
        lax.psum_scatter(gate_up_term.astype(jnp.bfloat16), "dp", scatter_dimension=0, tiled=True)
        .reshape(gate_up_weight.shape)
        .astype(jnp.float32)
    )
    grad_down = down_sum.T
    resid_part, gain_two_term = rms_backward(d_normed_two, scaled_two, inverse_two, gain_two)
    d_resid = cotangent.reshape(local_rows, width).astype(jnp.float32) + resid_part
    d_resid16 = lax.all_gather(
        d_resid.astype(jnp.bfloat16).reshape(seqs_here, local_len, width), "seq", axis=1, tiled=True
    ).reshape(total_rows, width)
    d_attended = times_transpose(d_resid16, out_rows).astype(jnp.bfloat16)
    d_attended = d_attended.reshape(seqs_here, full_len, kv_local, groups, HEAD_DIM)
    scores = masked_scores()
    probs = jnp.exp(scores - log_total)
    d_probs = jnp.einsum(
        "sqgjd,skgd->sgjqk", d_attended, value16, preferred_element_type=jnp.float32
    )
    delta = jnp.sum(probs * d_probs, axis=-1, keepdims=True)
    d_scores16 = (probs * (d_probs - delta) * score_scale).astype(jnp.bfloat16)
    d_query = jnp.einsum("sgjqk,skgd->sqgjd", d_scores16, key16, preferred_element_type=jnp.float32)
    d_key = jnp.einsum(
        "sgjqk,sqgjd->skgd", d_scores16, query_groups, preferred_element_type=jnp.float32
    )
    d_value = jnp.einsum(
        "sgjqk,sqgjd->skgd", probs16, d_attended, preferred_element_type=jnp.float32
    )
    d_query = unrotate(
        d_query.reshape(seqs_here, full_len, kv_local * groups, HEAD_DIM), cosine, sine
    )
    d_query = d_query.reshape(seqs_here, full_len, kv_local, groups, HEAD_DIM)
    d_key = unrotate(d_key, cosine, sine)
    d_qkv16 = jnp.concatenate([d_query, d_key[:, :, :, None], d_value[:, :, :, None]], 3)
    d_qkv16 = d_qkv16.reshape(total_rows, qkv_cols.shape[1]).astype(jnp.bfloat16)
    d_normed_one = to_local(times_transpose(d_qkv16, qkv_cols))
    qkv_term = contract_rows(normed_one, d_qkv16)
    out_term = contract_rows(d_resid16, attended16)
    grad_qkv = lax.psum_scatter(
        qkv_term.astype(jnp.bfloat16), "dp", scatter_dimension=0, tiled=True
    ).astype(jnp.float32)
    out_sum = lax.psum_scatter(
        out_term.astype(jnp.bfloat16), "dp", scatter_dimension=0, tiled=True
    ).astype(jnp.float32)
    grad_out = out_sum.T
    input_part, gain_one_term = rms_backward(d_normed_one, scaled_one, inverse_one, gain_one)
    input_grad = (d_resid + input_part).astype(jnp.bfloat16).reshape(block_input.shape)
    gain_grads = lax.psum_scatter(
        jnp.stack([gain_one_term, gain_two_term], 1), ("dp", "seq"), scatter_dimension=0, tiled=True
    )
    grad_gain_one = gain_grads[:, 0]
    grad_gain_two = gain_grads[:, 1]
    w_one, m_one, v_one = adam_update(attn_gain, grad_gain_one, first_attn_gain, second_attn_gain)
    w_qkv, m_qkv, v_qkv = adam_update(qkv_weight, grad_qkv, first_qkv, second_qkv)
    w_out, m_out, v_out = adam_update(out_weight, grad_out, first_out, second_out)
    w_two, m_two, v_two = adam_update(mlp_gain, grad_gain_two, first_mlp_gain, second_mlp_gain)
    w_gu, m_gu, v_gu = adam_update(gate_up_weight, grad_gate_up, first_gate_up, second_gate_up)
    w_down, m_down, v_down = adam_update(down_weight, grad_down, first_down, second_down)
    return (
        output,
        input_grad,
        grad_gain_one,
        grad_qkv,
        grad_out,
        grad_gain_two,
        grad_gate_up,
        grad_down,
        w_one,
        w_qkv,
        w_out,
        w_two,
        w_gu,
        w_down,
        m_one,
        m_qkv,
        m_out,
        m_two,
        m_gu,
        m_down,
        v_one,
        v_qkv,
        v_out,
        v_two,
        v_gu,
        v_down,
    )


def solution(mesh):
    in_specs = (
        P("dp", "seq", None),
        P("dp", None),
        P("dp", "seq", None),
        P(("dp", "seq")),
        P("dp", "seq"),
        P("seq", "dp"),
        P(("dp", "seq")),
        P("dp", None, "seq"),
        P("seq", "dp"),
        P(("dp", "seq")),
        P("dp", "seq"),
        P("seq", "dp"),
        P(("dp", "seq")),
        P("dp", None, "seq"),
        P("seq", "dp"),
        P(("dp", "seq")),
        P("dp", "seq"),
        P("seq", "dp"),
        P(("dp", "seq")),
        P("dp", None, "seq"),
        P("seq", "dp"),
    )
    out_specs = (
        P("dp", "seq", None),
        P("dp", "seq", None),
        P(("dp", "seq")),
        P("dp", "seq"),
        P("seq", "dp"),
        P(("dp", "seq")),
        P("dp", None, "seq"),
        P("seq", "dp"),
        P(("dp", "seq")),
        P("dp", "seq"),
        P("seq", "dp"),
        P(("dp", "seq")),
        P("dp", None, "seq"),
        P("seq", "dp"),
        P(("dp", "seq")),
        P("dp", "seq"),
        P("seq", "dp"),
        P(("dp", "seq")),
        P("dp", None, "seq"),
        P("seq", "dp"),
        P(("dp", "seq")),
        P("dp", "seq"),
        P("seq", "dp"),
        P(("dp", "seq")),
        P("dp", None, "seq"),
        P("seq", "dp"),
    )
    return jax.shard_map(
        per_device, mesh=mesh, in_specs=in_specs, out_specs=out_specs, check_vma=False
    )
```

profile of v0, /device:TPU:0, one launch (start us, length us, event | category | flops | bytes accessed | tf_op | source)
XLA Modules:
  0.0 1514.0 jit_solution(13102967327842110868)
XLA Ops:
  7.3 2.0 convert_element_type.162
  10.0 69.8 %all-gather = bf16[32,64,2]{1,2,0:T(2,128)(2,1)S(1)} all-gather(bf16[1,64,2]{1,2,0:T(2,128)(2,1)S(1)} %maximum_bitcast_fusion.4), channel_id=1, replica_groups=mesh['dp'=8,'seq'=4] {'dp','seq'}, dimensions={0}, use_global_device_ids=true | all-gather | bytes 8448 | tf_op jit(solution)/shard_map/all_gather | solution.py:132
  79.9 1.5 fusion.32
  81.5 2.5 fusion.29
  86.3 4.8 copy.86
  91.1 70.0 %all-gather.10.cloned.1.call-done = bf16[2,512,2048]{2,1,0:T(8,128)(2,1)} async-done(((bf16[2,128,2048]{2,1,0:T(8,128)(2,1)}), bf16[2,512,2048]{2,1,0:T(8,128)(2,1)}) %all-gather.10.cloned.1.call-update) | async-done | bytes 4194320 | tf_op jit(solution)/shard_map/all_gather | solution.py:137
  161.2 6.3 fusion.9
  169.2 7.4 fusion.5
  176.6 9.6 exponential_reduce_fusion
  186.2 10.3 fusion.35
  196.5 1.1 copy.88
  197.9 6.4 convolution_convert_fusion.2
  204.3 75.1 %reduce-scatter.12.cloned.1.call-done = bf16[2,128,2048]{2,1,0:T(8,128)(2,1)} async-done(((bf16[2,512,2048]{2,1,0:T(8,128)(2,1)}), bf16[2,128,2048]{2,1,0:T(8,128)(2,1)}) %reduce-scatter.12.cloned.1.call-update) | async-done | bytes 1048592 | tf_op jit(solution)/shard_map/reduce_scatter | solution.py:184
  279.4 1.6 multiply_reduce_fusion
  281.0 2.6 multiply_convert_fusion.3
  283.7 4.2 convert_element_type.174
  287.9 2.2 copy.122
  292.1 72.9 %all-gather.16.cloned.1.call-done = bf16[2,512,2048]{2,1,0:T(8,128)(2,1)} async-done(((bf16[2,128,2048]{2,1,0:T(8,128)(2,1)}), bf16[2,512,2048]{2,1,0:T(8,128)(2,1)}) %all-gather.16.cloned.1.call-update) | async-done | bytes 4194320 | tf_op jit(solution)/shard_map/all_gather | solution.py:196
  365.0 90.6 %all-gather.18.cloned.1.call-done = bf16[2048,4096]{1,0:T(8,128)(2,1)} async-done(((bf16[256,4096]{1,0:T(8,128)(2,1)}), bf16[2048,4096]{1,0:T(8,128)(2,1)}) %all-gather.18.cloned.1.call-update) | async-done | bytes 16777232 | tf_op jit(solution)/shard_map/all_gather | solution.py:142
  455.6 23.9 %fusion.71 = f32[1024,4096]{1,0:T(8,128)} fusion(bf16[1024,2048]{1,0:T(8,128)(2,1)} %bitcast.221, bf16[2048,4096]{1,0:T(8,128)(2,1)} %all-gather.18.cloned.1.call-done), kind=kOutput, calls=%fused_computation.139 | convolution fusion | flops 17179869184 | bytes 37748736 | tf_op jit(solution)/shard_map/dot_general | solution.py:199
  479.5 58.4 %all-gather.22.cloned.1.call-done = bf16[2,512,2048]{2,1,0:T(8,128)(2,1)} async-done(((bf16[2,128,2048]{2,1,0:T(8,128)(2,1)}), bf16[2,512,2048]{2,1,0:T(8,128)(2,1)}) %all-gather.22.cloned.1.call-update) | async-done | bytes 4194320 | tf_op jit(solution)/shard_map/all_gather | solution.py:145
  538.0 56.8 %all-gather.20.cloned.1.call-done = bf16[2048,2048]{1,0:T(8,128)(2,1)} async-done(((bf16[2048,256]{1,0:T(8,128)(2,1)}), bf16[2048,2048]{1,0:T(8,128)(2,1)}) %all-gather.20.cloned.1.call-update) | async-done | bytes 8388624 | tf_op jit(solution)/shard_map/all_gather | solution.py:146
  594.8 21.7 %multiply_convert_fusion.1 = (bf16[1024,2048]{1,0:T(8,128)(2,1)}, bf16[1024,2048]{1,0:T(8,128)(2,1)}, bf16[1024,2048]{1,0:T(8,128)(2,1)}) fusion(f32[1024,4096]{1,0:T(8,128)} %fusion.71, bf16[1024,2048]{1,0:T(8,128)(2,1)} %bitcast.223, bf16[2048,2048]{1,0:T(8,128)(2,1)} %all-gather.20.cloned.1.call-done), kind=kOutput, calls=%fused_computation.15 | convolution fusion | flops 8621391872 | bytes 41943040 | tf_op jit(solution)/shard_map/dot_general | solution.py:93
  616.5 23.8 %fusion.11 = bf16[1024,2048]{1,0:T(8,128)(2,1)} fusion(bf16[2048,4096]{1,0:T(8,128)(2,1)} %all-gather.18.cloned.1.call-done, bf16[1024,2048]{1,0:T(8,128)(2,1)} %get-tuple-element.129, bf16[1024,2048]{1,0:T(8,128)(2,1)} %get-tuple-element.128), kind=kOutput, calls=%fused_computation.26 | convolution fusion | flops 17198743552 | bytes 29360128 | tf_op jit(solution)/shard_map/dot_general | solution.py:93
  640.6 76.7 %reduce-scatter.16.cloned.1.call-done = bf16[2,128,2048]{2,1,0:T(8,128)(2,1)} async-done(((bf16[2,512,2048]{2,1,0:T(8,128)(2,1)}), bf16[2,128,2048]{2,1,0:T(8,128)(2,1)}) %reduce-scatter.16.cloned.1.call-update) | async-done | bytes 1048592 | tf_op jit(solution)/shard_map/reduce_scatter | solution.py:184
  717.3 2.0 fusion.28
  719.4 3.2 fusion.38
  722.7 81.3 %all-gather.24.cloned.1.call-done = bf16[2,512,2048]{2,1,0:T(8,128)(2,1)} async-done(((bf16[2,128,2048]{2,1,0:T(8,128)(2,1)}), bf16[2,512,2048]{2,1,0:T(8,128)(2,1)}) %all-gather.24.cloned.1.call-update) | async-done | bytes 4194320 | tf_op jit(solution)/shard_map/all_gather | solution.py:226
  804.0 6.2 convolution_convert_fusion.7
  810.2 4.6 reshape.347
  814.8 4.0 copy.90
  818.9 9.5 fusion.42
  828.4 24.6 %fusion.18 = f32[2,2,64,4,512]{4,2,3,1,0:T(8,128)} fusion(f32[2,2,512,512,4]{3,2,4,1,0:T(8,128)} %fusion.42, f32[2,2,512,512,4]{3,2,4,1,0:T(8,128)} %get-tuple-element.148, f32[2,2,4,512]{3,2,1,0:T(4,128)S(1)} %bitcast.215, pred[2,512,512]{1,2,0:T(8,128)(4,1)} %copy-done.10, bf16[2,512,2,32]{1,3,2,0:T(8,128)(2,1)S(1)} %get-tuple-element.140, ...), kind=kOutput, calls=%fused_computation.42 | convolution fusion | flops 583541248 | bytes 36470784 | tf_op jit(solution)/shard_map/sgjqk,skgd->sqgjd/dot_general | solution.py:238
  853.0 24.9 %fusion.36 = f32[2,512,2,64]{1,3,2,0:T(8,128)} fusion(f32[2,2,512,512,4]{3,2,4,1,0:T(8,128)} %fusion.42, f32[2,2,512,512,4]{3,2,4,1,0:T(8,128)} %get-tuple-element.148, f32[2,2,4,512]{3,2,1,0:T(4,128)S(1)} %bitcast.216, pred[2,512,512]{1,2,0:T(8,128)(4,1)} %copy-done.10, bf16[2,512,2,4,32]{1,4,3,2,0:T(8,128)(2,1)} %bitcast.201, ...), kind=kOutput, calls=%fused_computation.75 | convolution fusion | flops 585114112 | bytes 35684352 | tf_op jit(solution)/shard_map/sgjqk,sqgjd->skgd/dot_general | solution.py:239
  877.9 10.3 convolution_bitcast_fusion
  890.5 6.1 maximum_convert_fusion
  897.1 5.0 convolution_convert_fusion.3
  902.2 14.5 convert_bitcast_fusion
  916.8 6.2 convolution_convert_fusion.5
  923.1 7.9 convolution_convert_fusion.4
  931.1 14.0 convolution_convert_fusion.1
  945.2 32.4 %reduce-scatter.18.cloned.1.call-done = bf16[2,128,2048]{2,1,0:T(8,128)(2,1)} async-done(((bf16[2,512,2048]{2,1,0:T(8,128)(2,1)}), bf16[2,128,2048]{2,1,0:T(8,128)(2,1)}) %reduce-scatter.18.cloned.1.call-update) | async-done | bytes 1048592 | tf_op jit(solution)/shard_map/reduce_scatter | solution.py:184
  977.6 1.9 fusion.31
  979.6 1.3 copy.115
  981.0 25.4 %convolution_convert_fusion = bf16[2048,4096]{1,0:T(8,128)(2,1)} fusion(bf16[1024,2048]{1,0:T(8,128)(2,1)} %bitcast.222, bf16[1024,2048]{1,0:T(8,128)(2,1)} %get-tuple-element.129, bf16[1024,2048]{1,0:T(8,128)(2,1)} %get-tuple-element.128), kind=kOutput, calls=%fused_computation.9 | convolution fusion | flops 17205035008 | bytes 29360128 | tf_op jit(solution)/shard_map/dot_general | solution.py:87
  1006.4 2.2 copy.101
  1008.6 2.0 copy.98
  1010.7 2.0 copy.99
  1012.7 40.1 %reduce-scatter.26.cloned.1.call-done = bf16[256,2048]{0,1:T(8,128)(2,1)} async-done(((bf16[2048,2048]{0,1:T(8,128)(2,1)}), bf16[256,2048]{0,1:T(8,128)(2,1)}) %reduce-scatter.26.cloned.1.call-update) | async-done | bytes 1048592 | tf_op jit(solution)/shard_map/reduce_scatter | solution.py:215
  1052.8 6.9 multiply_subtract_fusion.1
  1059.6 37.5 %reduce-scatter.22.cloned.1.call-done = bf16[256,512]{1,0:T(8,128)(2,1)} async-done(((bf16[2048,512]{1,0:T(8,128)(2,1)}), bf16[256,512]{1,0:T(8,128)(2,1)}) %reduce-scatter.22.cloned.1.call-update) | async-done | bytes 262160 | tf_op jit(solution)/shard_map/reduce_scatter | solution.py:258
  1097.2 2.9 multiply_subtract_fusion.4
  1100.1 2.0 copy.103
  1102.1 2.0 copy.104
  1104.2 2.0 copy.105
  1107.0 2.1 copy.102
  1109.1 37.4 %reduce-scatter.20.cloned.1.call-done = bf16[256,768]{1,0:T(8,128)(2,1)} async-done(((bf16[2048,768]{1,0:T(8,128)(2,1)}), bf16[256,768]{1,0:T(8,128)(2,1)}) %reduce-scatter.20.cloned.1.call-update) | async-done | bytes 393232 | tf_op jit(solution)/shard_map/reduce_scatter | solution.py:255
  1146.5 3.5 multiply_subtract_fusion.3
  1150.1 75.4 %reduce-scatter.14.cloned.1.call-done = bf16[2,128,2048]{2,1,0:T(8,128)(2,1)} async-done(((bf16[2,512,2048]{2,1,0:T(8,128)(2,1)}), bf16[2,128,2048]{2,1,0:T(8,128)(2,1)}) %reduce-scatter.14.cloned.1.call-update) | async-done | bytes 1048592 | tf_op jit(solution)/shard_map/reduce_scatter | solution.py:184
  1225.5 4.9 fusion.24
  1230.4 135.3 %reduce-scatter.28.cloned.1.call-done = f32[64,2]{1,0:T(8,128)} async-done(((f32[2048,2]{1,0:T(8,128)}), f32[64,2]{1,0:T(8,128)}) %reduce-scatter.28.cloned.1.call-update) | async-done | bytes 528
  1367.9 113.8 %reduce-scatter.24.cloned.1.call-done = bf16[256,4096]{1,0:T(8,128)(2,1)} async-done(((bf16[2048,4096]{1,0:T(8,128)(2,1)}), bf16[256,4096]{1,0:T(8,128)(2,1)}) %reduce-scatter.24.cloned.1.call-update) | async-done | bytes 2097168 | tf_op jit(solution)/shard_map/reduce_scatter | solution.py:219
  1481.7 6.6 reshape.336
  1488.3 18.9 %multiply_subtract_fusion = (f32[256,2,2048]{2,1,0:T(2,128)}, f32[256,2,2048]{2,1,0:T(2,128)}, f32[256,2,2048]{2,1,0:T(2,128)}) fusion(f32[256,2,2048]{2,1,0:T(2,128)} %param.28, f32[256,2,2048]{2,1,0:T(2,128)} %reshape.336, f32[256,2,2048]{2,1,0:T(2,128)} %param.34, f32[256,2,2048]{2,1,0:T(2,128)} %param.40), kind=kLoop, calls=%fused_computation.24 | loop fusion | flops 15728640 | bytes 29360128 | tf_op jit(solution)/shard_map/sub | solution.py:80
  (138 shorter events, 13.5 us)
Async XLA Ops:
  7.2 76.8 %copy-start.11 = (f32[512,256]{1,0:T(8,128)S(1)}, f32[512,256]{1,0:T(8,128)}, u32[]{:S(2)}) copy-start(f32[512,256]{1,0:T(8,128)} %param.26) | copy-start | bytes 1572868
  7.2 77.8 %copy-start.21 = (s32[2,512]{1,0:T(2,128)S(1)}, s32[2,512]{1,0:T(2,128)}, u32[]{:S(2)}) copy-start(s32[2,512]{1,0:T(2,128)} %param.22) | copy-start | bytes 12292
  7.2 79.1 %all-gather.12.cloned.1.call-start = ((), (), s32[]{:S(2)}) async-start(), calls=%async_computation.10 | async-start | bytes 3538944 | tf_op jit(solution)/shard_map/all_gather | solution.py:140
  9.3 151.9 %all-gather.10.cloned.1.call-start = ((), (), s32[]{:S(2)}) async-start(), calls=%async_computation.9 | async-start | bytes 5242880 | tf_op jit(solution)/shard_map/all_gather | solution.py:137
  81.4 3.8 copy-start.22
  81.5 3.8 copy-start.19
  84.0 113.9 %all-gather.14.cloned.1.call-start = ((), (), s32[]{:S(2)}) async-start(), calls=%async_computation.11 | async-start | bytes 2359296 | tf_op jit(solution)/shard_map/all_gather | solution.py:141
  84.8 194.6 %reduce-scatter.12.cloned.1.call-start = ((), (), s32[]{:S(2)}) async-start(), calls=%async_computation.12 | async-start | bytes 5242880 | tf_op jit(solution)/shard_map/reduce_scatter | solution.py:184
  85.7 100.4 %copy-start.10 = (pred[2,512,512]{1,2,0:T(8,128)(4,1)}, pred[2,512,512]{1,2,0:T(8,128)(4,1)S(1)}, u32[]{:S(2)}) copy-start(pred[2,512,512]{1,2,0:T(8,128)(4,1)S(1)} %compare_and_fusion) | copy-start | bytes 1572868
  86.3 81.5 %copy-start.4 = (f32[2,512,32]{1,2,0:T(8,128)}, f32[2,512,32]{1,2,0:T(8,128)S(1)}, u32[]{:S(2)}) copy-start(f32[2,512,32]{1,2,0:T(8,128)S(1)} %get-tuple-element.145) | copy-start | bytes 393220
  86.3 81.5 %copy-start.6 = (f32[2,512,32]{1,2,0:T(8,128)}, f32[2,512,32]{1,2,0:T(8,128)S(1)}, u32[]{:S(2)}) copy-start(f32[2,512,32]{1,2,0:T(8,128)S(1)} %get-tuple-element.146) | copy-start | bytes 393220
  167.5 1.7 copy-start.9
  169.2 7.4 copy-start.17
  169.2 7.4 copy-start.18
  197.9 6.4 copy-start.14
  204.2 75.1 %copy-start = (bf16[2,128,2048]{2,1,0:T(8,128)(2,1)S(1)}, bf16[2,128,2048]{2,1,0:T(8,128)(2,1)}, u32[]{:S(2)}) copy-start(bf16[2,128,2048]{2,1,0:T(8,128)(2,1)} %param.21) | copy-start | bytes 3145732
  204.3 160.8 %all-gather.16.cloned.1.call-start = ((), (), s32[]{:S(2)}) async-start(), calls=%async_computation.13 | async-start | bytes 5242880 | tf_op jit(solution)/shard_map/all_gather | solution.py:196
  283.7 172.0 %all-gather.18.cloned.1.call-start = ((), (), s32[]{:S(2)}) async-start(), calls=%async_computation.14 | async-start | bytes 18874368 | tf_op jit(solution)/shard_map/all_gather | solution.py:142
  287.9 3.1 copy-start.3
  290.2 247.8 %all-gather.22.cloned.1.call-start = ((), (), s32[]{:S(2)}) async-start(), calls=%async_computation.17 | async-start | bytes 5242880 | tf_op jit(solution)/shard_map/all_gather | solution.py:145
  290.9 303.9 %all-gather.20.cloned.1.call-start = ((), (), s32[]{:S(2)}) async-start(), calls=%async_computation.15 | async-start | bytes 9437184 | tf_op jit(solution)/shard_map/all_gather | solution.py:146
  292.1 425.2 %reduce-scatter.16.cloned.1.call-start = ((), (), s32[]{:S(2)}) async-start(), calls=%async_computation.18 | async-start | bytes 5242880 | tf_op jit(solution)/shard_map/reduce_scatter | solution.py:184
  640.3 77.0 %copy-start.1 = (bf16[2,128,2048]{2,1,0:T(8,128)(2,1)S(1)}, bf16[2,128,2048]{2,1,0:T(8,128)(2,1)}, u32[]{:S(2)}) copy-start(bf16[2,128,2048]{2,1,0:T(8,128)(2,1)} %reduce-scatter.12.cloned.1.call-done) | copy-start | bytes 3145732
  640.3 79.0 %copy-start.2 = (bf16[2,128,2048]{2,1,0:T(8,128)(2,1)S(1)}, bf16[2,128,2048]{2,1,0:T(8,128)(2,1)}, u32[]{:S(2)}) copy-start(bf16[2,128,2048]{2,1,0:T(8,128)(2,1)} %param.23) | copy-start | bytes 3145732
  640.4 163.6 %all-gather.24.cloned.1.call-start = ((), (), s32[]{:S(2)}) async-start(), calls=%async_computation.19 | async-start | bytes 5242880 | tf_op jit(solution)/shard_map/all_gather | solution.py:226
  722.6 255.0 %reduce-scatter.18.cloned.1.call-start = ((), (), s32[]{:S(2)}) async-start(), calls=%async_computation.20 | async-start | bytes 5242880 | tf_op jit(solution)/shard_map/reduce_scatter | solution.py:184
  877.9 10.4 copy-start.5
  877.9 10.4 copy-start.7
  877.9 10.3 copy-start.12
  888.2 1.6 copy-start.16
  889.9 7.2 copy-start.8
  897.1 5.1 copy-start.13
  902.2 150.6 %reduce-scatter.26.cloned.1.call-start = ((), (), s32[]{:S(2)}) async-start(), calls=%async_computation.24 | async-start | bytes 9437184 | tf_op jit(solution)/shard_map/reduce_scatter | solution.py:215
  916.8 180.4 %reduce-scatter.22.cloned.1.call-start = ((), (), s32[]{:S(2)}) async-start(), calls=%async_computation.22 | async-start | bytes 2359296 | tf_op jit(solution)/shard_map/reduce_scatter | solution.py:258
  923.0 223.5 %reduce-scatter.20.cloned.1.call-start = ((), (), s32[]{:S(2)}) async-start(), calls=%async_computation.21 | async-start | bytes 3538944 | tf_op jit(solution)/shard_map/reduce_scatter | solution.py:255
  931.0 294.5 %reduce-scatter.14.cloned.1.call-start = ((), (), s32[]{:S(2)}) async-start(), calls=%async_computation.16 | async-start | bytes 5242880 | tf_op jit(solution)/shard_map/reduce_scatter | solution.py:184
  945.1 32.5 %copy-start.20 = (f32[1,2048]{1,0:T(1,128)S(1)}, f32[1,2048]{1,0:T(1,128)}, u32[]{:S(2)}) copy-start(f32[1,2048]{1,0:T(1,128)} %copy-done.19) | copy-start | bytes 24580
  945.1 32.5 %copy-start.23 = (f32[2,128]{1,0:T(2,128)S(1)}, f32[2,128]{1,0:T(2,128)}, u32[]{:S(2)}) copy-start(f32[2,128]{1,0:T(2,128)} %copy-done.22) | copy-start | bytes 3076
  945.1 420.6 %reduce-scatter.28.cloned.1.call-start = ((), (), s32[]{:S(2)}) async-start(), calls=%async_computation.25 | async-start | bytes 1081344
  981.0 500.8 %reduce-scatter.24.cloned.1.call-start = ((), (), s32[]{:S(2)}) async-start(), calls=%async_computation.23 | async-start | bytes 18874368 | tf_op jit(solution)/shard_map/reduce_scatter | solution.py:219
  1097.2 9.0 copy-start.15
  1150.0 216.7 %copy-start.26 = (f32[64]{0:T(128)S(1)}, f32[64]{0:T(128)}, u32[]{:S(2)}) copy-start(f32[64]{0:T(128)} %param.27) | copy-start | bytes 772
  1150.0 216.7 %copy-start.28 = (f32[64]{0:T(128)S(1)}, f32[64]{0:T(128)}, u32[]{:S(2)}) copy-start(f32[64]{0:T(128)} %param.33) | copy-start | bytes 772
  1150.0 216.7 %copy-start.29 = (f32[64]{0:T(128)S(1)}, f32[64]{0:T(128)}, u32[]{:S(2)}) copy-start(f32[64]{0:T(128)} %param.39) | copy-start | bytes 772
  1150.0 217.3 %copy-start.27 = (f32[64]{0:T(128)S(1)}, f32[64]{0:T(128)}, u32[]{:S(2)}) copy-start(f32[64]{0:T(128)} %param.24) | copy-start | bytes 772
  1150.1 217.3 %copy-start.30 = (f32[64]{0:T(128)S(1)}, f32[64]{0:T(128)}, u32[]{:S(2)}) copy-start(f32[64]{0:T(128)} %param.30) | copy-start | bytes 772
  1150.1 217.3 %copy-start.31 = (f32[64]{0:T(128)S(1)}, f32[64]{0:T(128)}, u32[]{:S(2)}) copy-start(f32[64]{0:T(128)} %param.36) | copy-start | bytes 772
  1366.7 140.5 %copy-start.24 = (f32[64,1]{0,1:T(1,128)}, f32[64,1]{0,1:T(1,128)S(1)}, u32[]{:S(2)}) copy-start(f32[64,1]{0,1:T(1,128)S(1)} %copy.120) | copy-start | bytes 772
  1366.8 140.4 %copy-start.25 = (f32[64,1]{0,1:T(1,128)}, f32[64,1]{0,1:T(1,128)S(1)}, u32[]{:S(2)}) copy-start(f32[64,1]{0,1:T(1,128)S(1)} %copy.119) | copy-start | bytes 772
Sparse Core Ops, SparseCore 0:
  10.5 34.9 all-gather.11
  84.1 76.9 all-gather.9
  163.6 26.5 all-gather.13
  204.4 74.9 reduce-scatter.11
  283.8 81.2 all-gather.15
  367.4 88.2 all-gather.17
  457.2 80.7 all-gather.21
  540.4 54.3 all-gather.19
  640.5 76.7 reduce-scatter.15
  722.7 81.2 all-gather.23
  902.3 75.2 reduce-scatter.17
  980.9 71.7 reduce-scatter.25
  1056.1 41.0 reduce-scatter.21
  1100.4 46.0 reduce-scatter.19
  1148.6 76.7 reduce-scatter.13
  1228.1 137.5 reduce-scatter.27
  1369.1 112.5 reduce-scatter.23
where the time goes:
time: 1520 us; the launch traced here: 1510 us
  waiting for transfers between devices  1050 us (69%)
  matrix products  248 us (16%)
  other arithmetic  81.3 us (5%)
  blocking collectives  69.8 us (5%)
  local copies, waits for them, and re-layouts  43.9 us (3%)
    reduce_scatter x4, waiting for transfers between devices, to_local(): lax.psum_scatter(part.astype(jnp.bfloat16).reshape(seqs_here, full_len, w...  260 us
    unnamed x18, waiting for transfers between devices  136 us
    reduce_scatter x1, waiting for transfers between devices, per_device(): lax.psum_scatter(gate_up_term.astype(jnp.bfloat16), 'dp', scatter_dimensi...  114 us
    all_gather x1, waiting for transfers between devices, per_device(): lax.all_gather(gate_up_weight.astype(jnp.bfloat16).reshape(-1, 2 * unit_c...  90.6 us
    all_gather x1, waiting for transfers between devices, per_device(): lax.all_gather(d_resid.astype(jnp.bfloat16).reshape(seqs_here, local_len,...  81.3 us
    all_gather x1, waiting for transfers between devices, per_device(): lax.all_gather(normed_two_here.reshape(seqs_here, local_len, width), 'seq...  72.9 us
    all_gather x1, waiting for transfers between devices, per_device(): lax.all_gather(normed_here.reshape(seqs_here, local_len, width), 'seq', a...  70 us
    all_gather x1, blocking collectives, per_device(): gain_block = lax.all_gather(gain_pair, ('dp', 'seq'), axis=1, tiled=True)  69.8 us
  transfers between devices with their start and end apart: 17, of which 15 were waited for; matrix products, arithmetic and copies ran while one was open for 12% of the time, Pallas kernels for 0%

commit v1 on v0

--- a/solution.py
+++ b/solution.py
@@ -15,6 +15,23 @@
 adam_eps = 1e-08
 step_count = 10.0
 masked_score = -1e30
+
+
+def quarters_fit(view, ndim_at):
+    along_axis = "dp"
+    work_now = lax.axis_size(along_axis)
+    all_rows = lax.axis_index(along_axis)
+    q_next, heard = (work_now, all_rows)
+    inter, u_next = (view, 1)
+    while u_next < q_next:
+        kept_arr = lax.ppermute(
+            inter, along_axis, perm=tuple(((u, u ^ u_next) for u in range(q_next)))
+        )
+        arr_out = jnp.concatenate([inter, kept_arr], axis=ndim_at)
+        right_arr = jnp.concatenate([kept_arr, inter], axis=ndim_at)
+        inter = jnp.where(heard & u_next == 0, arr_out, right_arr)
+        u_next = 2 * u_next
+    return inter
 
 
 def segment_positions(segments):
@@ -139,9 +156,7 @@
     ).reshape(total_rows, width)
     qkv_cols = lax.all_gather(qkv_weight.astype(jnp.bfloat16), "dp", axis=0, tiled=True)
     out_rows = lax.all_gather(out_weight.astype(jnp.bfloat16), "dp", axis=1, tiled=True)
-    gate_up_cols = lax.all_gather(
-        gate_up_weight.astype(jnp.bfloat16).reshape(-1, 2 * unit_count), "dp", axis=0, tiled=True
-    )
+    gate_up_cols = quarters_fit(gate_up_weight.astype(jnp.bfloat16).reshape(-1, 2 * unit_count), 0)
     cot_all = lax.all_gather(cotangent, "seq", axis=1, tiled=True)
     down_rows = lax.all_gather(down_weight.astype(jnp.bfloat16), "dp", axis=1, tiled=True)
     positions = segment_positions(segment_ids)

time: 1520 us -> 1570 us (1.033)
  waiting for transfers between devices: 1050 us -> 1090 us
  other arithmetic: 81.3 us -> 97.1 us
    ppermute x0 -> x3, waiting for transfers between devices: none -> 309 us  [quarters_fit(): lax.ppermute(inter, along_axis, perm=tuple(((u, u ^ u_next) for u in rang...]
    all_gather x1 -> x0, waiting for transfers between devices: 90.6 us -> none  [per_device(): lax.all_gather(gate_up_weight.astype(jnp.bfloat16).reshape(-1, 2 * unit_c...]
    all_gather x1, waiting for transfers between devices: 72.9 us -> 0.01 us  [per_device(): lax.all_gather(normed_two_here.reshape(seqs_here, local_len, width), 'seq...]
    all_gather x1, waiting for transfers between devices: 58.4 us -> 0.01 us  [per_device(): cot_all = lax.all_gather(cotangent, 'seq', axis=1, tiled=True)]
    all_gather x1, waiting for transfers between devices: 56.8 us -> 0.01 us  [per_device(): lax.all_gather(down_weight.astype(jnp.bfloat16), 'dp', axis=1, tiled=True)]
    select_n x0 -> x2, other arithmetic: none -> 15.8 us  [quarters_fit(): inter = jnp.where(heard & u_next == 0, arr_out, right_arr)]
    unnamed x18 -> x17, waiting for transfers between devices: 136 us -> 136 us
  transfers between devices with their start and end apart: 17 -> 19, of which waited for: 15 -> 14; matrix products, arithmetic and copies ran while one was open for 12% -> 13% of each run, Pallas kernels for 0% -> 0%
where the time goes in v1:
time: 1570 us
  waiting for transfers between devices  1090 us (69%)
  matrix products  252 us (16%)
  other arithmetic  97.1 us (6%)
  blocking collectives  69.8 us (4%)
  local copies, waits for them, and re-layouts  42.7 us (3%)
    ppermute x3, waiting for transfers between devices, quarters_fit(): lax.ppermute(inter, along_axis, perm=tuple(((u, u ^ u_next) for u in rang...  309 us
    reduce_scatter x4, waiting for transfers between devices, to_local(): lax.psum_scatter(part.astype(jnp.bfloat16).reshape(seqs_here, full_len, w...  260 us
    unnamed x17, waiting for transfers between devices  136 us
    reduce_scatter x1, waiting for transfers between devices, per_device(): lax.psum_scatter(gate_up_term.astype(jnp.bfloat16), 'dp', scatter_dimensi...  114 us
    all_gather x1, waiting for transfers between devices, per_device(): lax.all_gather(d_resid.astype(jnp.bfloat16).reshape(seqs_here, local_len,...  81.3 us
    all_gather x1, waiting for transfers between devices, per_device(): lax.all_gather(normed_here.reshape(seqs_here, local_len, width), 'seq', a...  70 us
    all_gather x1, blocking collectives, per_device(): gain_block = lax.all_gather(gain_pair, ('dp', 'seq'), axis=1, tiled=True)  69.8 us
    dot_general x4, matrix products, times_transpose(): lax.dot_general(left, right, (((1,), (1,)), ((), ())), preferred_element_...  58.3 us
  transfers between devices with their start and end apart: 19, of which 14 were waited for; matrix products, arithmetic and copies ran while one was open for 13% of the time, Pallas kernels for 0%

profile of v1, /device:TPU:0, one launch (start us, length us, event | category | flops | bytes accessed | tf_op | source)
XLA Modules:
  0.0 1566.0 jit_solution(11589303006721674715)
XLA Ops:
  7.3 2.0 convert_element_type.162
  10.0 69.8 %all-gather = bf16[32,64,2]{1,2,0:T(2,128)(2,1)S(1)} all-gather(bf16[1,64,2]{1,2,0:T(2,128)(2,1)S(1)} %maximum_bitcast_fusion.4), channel_id=1, replica_groups=mesh['dp'=8,'seq'=4] {'dp','seq'}, dimensions={0}, use_global_device_ids=true | all-gather | bytes 8448 | tf_op jit(solution)/shard_map/all_gather | solution.py:149
  79.9 1.5 fusion.33
  81.5 2.5 fusion.30
  86.3 4.8 copy.86
  91.1 70.0 %all-gather.9.cloned.1.call-done = bf16[2,512,2048]{2,1,0:T(8,128)(2,1)} async-done(((bf16[2,128,2048]{2,1,0:T(8,128)(2,1)}), bf16[2,512,2048]{2,1,0:T(8,128)(2,1)}) %all-gather.9.cloned.1.call-update) | async-done | bytes 4194320 | tf_op jit(solution)/shard_map/all_gather | solution.py:154
  161.2 6.3 fusion.9
  169.2 7.4 fusion.5
  176.6 9.6 exponential_reduce_fusion
  186.2 10.3 fusion.36
  197.9 6.4 convolution_convert_fusion.2
  204.8 74.6 %reduce-scatter.12.cloned.1.call-done = bf16[2,128,2048]{2,1,0:T(8,128)(2,1)} async-done(((bf16[2,512,2048]{2,1,0:T(8,128)(2,1)}), bf16[2,128,2048]{2,1,0:T(8,128)(2,1)}) %reduce-scatter.12.cloned.1.call-update) | async-done | bytes 1048592 | tf_op jit(solution)/shard_map/reduce_scatter | solution.py:199
  279.4 1.6 multiply_reduce_fusion
  281.0 2.6 multiply_convert_fusion.3
  284.3 4.2 convert_element_type.174
  289.5 4.3 collective-permute-done
  293.7 4.8 maximum_select_fusion.2
  298.6 1.5 collective-permute-start.1
  301.2 90.3 %collective-permute-done.1 = bf16[512,4096]{1,0:T(8,128)(2,1)} collective-permute-done((bf16[512,4096]{1,0:T(8,128)(2,1)}, bf16[512,4096]{1,0:T(8,128)(2,1)}, u32[]{:S(2)}, u32[]{:S(2)}) %collective-permute-start.1) | collective-permute-done | bytes 4194336 | tf_op jit(solution)/shard_map/ppermute | solution.py:27
  391.5 11.0 maximum_select_fusion.1
  402.5 1.5 collective-permute-start.2
  404.0 214.2 %collective-permute-done.2 = bf16[1024,4096]{1,0:T(8,128)(2,1)} collective-permute-done((bf16[1024,4096]{1,0:T(8,128)(2,1)}, bf16[1024,4096]{1,0:T(8,128)(2,1)}, u32[]{:S(2)}, u32[]{:S(2)}) %collective-permute-start.2) | collective-permute-done | bytes 8388640 | tf_op jit(solution)/shard_map/ppermute | solution.py:27
  618.2 25.4 %fusion.19 = f32[1024,4096]{1,0:T(8,128)} fusion(bf16[1024,2048]{1,0:T(8,128)(2,1)} %bitcast.220, bf16[1024,4096]{1,0:T(8,128)(2,1)} %collective-permute-done.2, bf16[1024,4096]{1,0:T(8,128)(2,1)} %maximum_select_fusion.1, pred[]{:T(512)S(6)} %eq.29), kind=kOutput, calls=%fused_computation.47 | convolution fusion | flops 17255366656 | bytes 37748736 | tf_op jit(solution)/shard_map/dot_general | solution.py:214
  643.6 21.8 %multiply_convert_fusion.1 = (bf16[1024,2048]{1,0:T(8,128)(2,1)}, bf16[1024,2048]{1,0:T(8,128)(2,1)}, bf16[1024,2048]{1,0:T(8,128)(2,1)}) fusion(f32[1024,4096]{1,0:T(8,128)} %fusion.19, bf16[1024,2048]{1,0:T(8,128)(2,1)} %bitcast.222, bf16[2048,2048]{1,0:T(8,128)(2,1)} %all-gather.17.cloned.1.call-done), kind=kOutput, calls=%fused_computation.17 | convolution fusion | flops 8621391872 | bytes 41943040 | tf_op jit(solution)/shard_map/dot_general | solution.py:110
  665.4 25.3 %fusion.11 = bf16[1024,2048]{1,0:T(8,128)(2,1)} fusion(bf16[1024,2048]{1,0:T(8,128)(2,1)} %get-tuple-element.129, bf16[1024,2048]{1,0:T(8,128)(2,1)} %get-tuple-element.128, bf16[1024,4096]{1,0:T(8,128)(2,1)} %collective-permute-done.2, bf16[1024,4096]{1,0:T(8,128)(2,1)} %maximum_select_fusion.1, pred[]{:T(512)S(6)} %eq.29), kind=kOutput, calls=%fused_computation.29 | convolution fusion | flops 17274241024 | bytes 29360128 | tf_op jit(solution)/shard_map/dot_general | solution.py:110
  690.8 77.4 %reduce-scatter.16.cloned.1.call-done = bf16[2,128,2048]{2,1,0:T(8,128)(2,1)} async-done(((bf16[2,512,2048]{2,1,0:T(8,128)(2,1)}), bf16[2,128,2048]{2,1,0:T(8,128)(2,1)}) %reduce-scatter.16.cloned.1.call-update) | async-done | bytes 1048592 | tf_op jit(solution)/shard_map/reduce_scatter | solution.py:199
  768.1 2.0 fusion.29
  770.2 3.2 fusion.39
  773.5 81.3 %all-gather.21.cloned.1.call-done = bf16[2,512,2048]{2,1,0:T(8,128)(2,1)} async-done(((bf16[2,128,2048]{2,1,0:T(8,128)(2,1)}), bf16[2,512,2048]{2,1,0:T(8,128)(2,1)}) %all-gather.21.cloned.1.call-update) | async-done | bytes 4194320 | tf_op jit(solution)/shard_map/all_gather | solution.py:241
  854.8 6.2 convolution_convert_fusion.7
  861.0 4.8 reshape.347
  865.8 4.0 copy.90
  869.9 9.6 fusion.43
  879.4 24.6 %fusion.18 = f32[2,2,64,4,512]{4,2,3,1,0:T(8,128)} fusion(f32[2,2,512,512,4]{3,2,4,1,0:T(8,128)} %fusion.43, f32[2,2,512,512,4]{3,2,4,1,0:T(8,128)} %get-tuple-element.148, f32[2,2,4,512]{3,2,1,0:T(4,128)S(1)} %bitcast.214, pred[2,512,512]{1,2,0:T(8,128)(4,1)} %copy-done.10, bf16[2,512,2,32]{1,3,2,0:T(8,128)(2,1)S(1)} %copy-done.22, ...), kind=kOutput, calls=%fused_computation.45 | convolution fusion | flops 583541248 | bytes 36470784 | tf_op jit(solution)/shard_map/sgjqk,skgd->sqgjd/dot_general | solution.py:253
  904.1 25.1 %fusion.37 = f32[2,512,2,64]{1,3,2,0:T(8,128)} fusion(f32[2,2,512,512,4]{3,2,4,1,0:T(8,128)} %fusion.43, f32[2,2,512,512,4]{3,2,4,1,0:T(8,128)} %get-tuple-element.148, f32[2,2,4,512]{3,2,1,0:T(4,128)S(1)} %bitcast.215, pred[2,512,512]{1,2,0:T(8,128)(4,1)} %copy-done.10, bf16[2,512,2,4,32]{1,4,3,2,0:T(8,128)(2,1)} %bitcast.200, ...), kind=kOutput, calls=%fused_computation.79 | convolution fusion | flops 585114112 | bytes 35684352 | tf_op jit(solution)/shard_map/sgjqk,sqgjd->skgd/dot_general | solution.py:254
  929.2 10.3 convolution_bitcast_fusion
  941.8 6.1 maximum_convert_fusion
  948.4 5.0 convolution_convert_fusion.3
  953.5 14.3 convert_bitcast_fusion
  967.8 6.3 convolution_convert_fusion.5
  974.2 7.9 convolution_convert_fusion.4
  982.2 14.1 convolution_convert_fusion.1
  996.3 32.6 %reduce-scatter.18.cloned.1.call-done = bf16[2,128,2048]{2,1,0:T(8,128)(2,1)} async-done(((bf16[2,512,2048]{2,1,0:T(8,128)(2,1)}), bf16[2,128,2048]{2,1,0:T(8,128)(2,1)}) %reduce-scatter.18.cloned.1.call-update) | async-done | bytes 1048592 | tf_op jit(solution)/shard_map/reduce_scatter | solution.py:199
  1028.9 1.9 fusion.32
  1032.3 25.4 %convolution_convert_fusion = bf16[2048,4096]{1,0:T(8,128)(2,1)} fusion(bf16[1024,2048]{1,0:T(8,128)(2,1)} %bitcast.221, bf16[1024,2048]{1,0:T(8,128)(2,1)} %get-tuple-element.129, bf16[1024,2048]{1,0:T(8,128)(2,1)} %get-tuple-element.128), kind=kOutput, calls=%fused_computation.10 | convolution fusion | flops 17205035008 | bytes 29360128 | tf_op jit(solution)/shard_map/dot_general | solution.py:104
  1057.7 2.2 copy.101
  1059.9 2.0 copy.98
  1062.0 2.0 copy.99
  1064.0 40.2 %reduce-scatter.26.cloned.1.call-done = bf16[256,2048]{0,1:T(8,128)(2,1)} async-done(((bf16[2048,2048]{0,1:T(8,128)(2,1)}), bf16[256,2048]{0,1:T(8,128)(2,1)}) %reduce-scatter.26.cloned.1.call-update) | async-done | bytes 1048592 | tf_op jit(solution)/shard_map/reduce_scatter | solution.py:230
  1104.2 6.9 multiply_subtract_fusion.1
  1111.1 37.4 %reduce-scatter.22.cloned.1.call-done = bf16[256,512]{1,0:T(8,128)(2,1)} async-done(((bf16[2048,512]{1,0:T(8,128)(2,1)}), bf16[256,512]{1,0:T(8,128)(2,1)}) %reduce-scatter.22.cloned.1.call-update) | async-done | bytes 262160 | tf_op jit(solution)/shard_map/reduce_scatter | solution.py:273
  1148.5 2.9 multiply_subtract_fusion.4
  1151.4 2.0 copy.103
  1153.4 2.0 copy.104
  1155.4 2.0 copy.105
  1158.3 2.1 copy.102
  1160.4 37.6 %reduce-scatter.20.cloned.1.call-done = bf16[256,768]{1,0:T(8,128)(2,1)} async-done(((bf16[2048,768]{1,0:T(8,128)(2,1)}), bf16[256,768]{1,0:T(8,128)(2,1)}) %reduce-scatter.20.cloned.1.call-update) | async-done | bytes 393232 | tf_op jit(solution)/shard_map/reduce_scatter | solution.py:270
  1197.9 3.5 multiply_subtract_fusion.3
  1201.5 75.4 %reduce-scatter.14.cloned.1.call-done = bf16[2,128,2048]{2,1,0:T(8,128)(2,1)} async-done(((bf16[2,512,2048]{2,1,0:T(8,128)(2,1)}), bf16[2,128,2048]{2,1,0:T(8,128)(2,1)}) %reduce-scatter.14.cloned.1.call-update) | async-done | bytes 1048592 | tf_op jit(solution)/shard_map/reduce_scatter | solution.py:199
  1276.9 4.9 fusion.25
  1281.8 135.4 %reduce-scatter.28.cloned.1.call-done = f32[64,2]{1,0:T(8,128)} async-done(((f32[2048,2]{1,0:T(8,128)}), f32[64,2]{1,0:T(8,128)}) %reduce-scatter.28.cloned.1.call-update) | async-done | bytes 528
  1419.4 114.1 %reduce-scatter.24.cloned.1.call-done = bf16[256,4096]{1,0:T(8,128)(2,1)} async-done(((bf16[2048,4096]{1,0:T(8,128)(2,1)}), bf16[256,4096]{1,0:T(8,128)(2,1)}) %reduce-scatter.24.cloned.1.call-update) | async-done | bytes 2097168 | tf_op jit(solution)/shard_map/reduce_scatter | solution.py:234
  1533.5 6.6 reshape.336
  1540.1 18.9 %multiply_subtract_fusion = (f32[256,2,2048]{2,1,0:T(2,128)}, f32[256,2,2048]{2,1,0:T(2,128)}, f32[256,2,2048]{2,1,0:T(2,128)}) fusion(f32[256,2,2048]{2,1,0:T(2,128)} %param.28, f32[256,2,2048]{2,1,0:T(2,128)} %reshape.336, f32[256,2,2048]{2,1,0:T(2,128)} %param.34, f32[256,2,2048]{2,1,0:T(2,128)} %param.40), kind=kLoop, calls=%fused_computation.27 | loop fusion | flops 15728640 | bytes 29360128 | tf_op jit(solution)/shard_map/sub | solution.py:97
  (151 shorter events, 16.9 us)
Async XLA Ops:
  7.2 76.8 %copy-start.11 = (f32[512,256]{1,0:T(8,128)S(1)}, f32[512,256]{1,0:T(8,128)}, u32[]{:S(2)}) copy-start(f32[512,256]{1,0:T(8,128)} %param.26) | copy-start | bytes 1572868
  7.2 77.8 %copy-start.25 = (s32[2,512]{1,0:T(2,128)S(1)}, s32[2,512]{1,0:T(2,128)}, u32[]{:S(2)}) copy-start(s32[2,512]{1,0:T(2,128)} %param.22) | copy-start | bytes 12292
  7.2 79.1 %all-gather.11.cloned.1.call-start = ((), (), s32[]{:S(2)}) async-start(), calls=%async_computation.10 | async-start | bytes 3538944 | tf_op jit(solution)/shard_map/all_gather | solution.py:157
  9.3 151.9 %all-gather.9.cloned.1.call-start = ((), (), s32[]{:S(2)}) async-start(), calls=%async_computation.9 | async-start | bytes 5242880 | tf_op jit(solution)/shard_map/all_gather | solution.py:154
  81.4 3.8 copy-start.26
  81.5 3.8 copy-start.23
  84.0 113.9 %all-gather.13.cloned.1.call-start = ((), (), s32[]{:S(2)}) async-start(), calls=%async_computation.11 | async-start | bytes 2359296 | tf_op jit(solution)/shard_map/all_gather | solution.py:158
  84.8 194.6 %reduce-scatter.12.cloned.1.call-start = ((), (), s32[]{:S(2)}) async-start(), calls=%async_computation.12 | async-start | bytes 5242880 | tf_op jit(solution)/shard_map/reduce_scatter | solution.py:199
  85.7 100.5 %copy-start.10 = (pred[2,512,512]{1,2,0:T(8,128)(4,1)}, pred[2,512,512]{1,2,0:T(8,128)(4,1)S(1)}, u32[]{:S(2)}) copy-start(pred[2,512,512]{1,2,0:T(8,128)(4,1)S(1)} %compare_and_fusion) | copy-start | bytes 1572868
  86.3 81.6 %copy-start.4 = (f32[2,512,32]{1,2,0:T(8,128)}, f32[2,512,32]{1,2,0:T(8,128)S(1)}, u32[]{:S(2)}) copy-start(f32[2,512,32]{1,2,0:T(8,128)S(1)} %get-tuple-element.145) | copy-start | bytes 393220
  86.3 81.6 %copy-start.6 = (f32[2,512,32]{1,2,0:T(8,128)}, f32[2,512,32]{1,2,0:T(8,128)S(1)}, u32[]{:S(2)}) copy-start(f32[2,512,32]{1,2,0:T(8,128)S(1)} %get-tuple-element.146) | copy-start | bytes 393220
  167.5 1.7 copy-start.9
  167.6 8.9 copy-start.19
  167.7 8.9 copy-start.21
  169.1 7.4 copy-start.17
  169.2 7.4 copy-start.18
  197.9 6.4 copy-start.14
  204.3 75.1 %copy-start = (bf16[2,128,2048]{2,1,0:T(8,128)(2,1)S(1)}, bf16[2,128,2048]{2,1,0:T(8,128)(2,1)}, u32[]{:S(2)}) copy-start(bf16[2,128,2048]{2,1,0:T(8,128)(2,1)} %param.21) | copy-start | bytes 3145732
  204.3 413.9 %all-gather.15.cloned.1.call-start = ((), (), s32[]{:S(2)}) async-start(), calls=%async_computation.13 | async-start | bytes 5242880 | tf_op jit(solution)/shard_map/all_gather | solution.py:211
  283.6 360.0 %all-gather.19.cloned.1.call-start = ((), (), s32[]{:S(2)}) async-start(), calls=%async_computation.16 | async-start | bytes 5242880 | tf_op jit(solution)/shard_map/all_gather | solution.py:160
  284.2 359.4 %all-gather.17.cloned.1.call-start = ((), (), s32[]{:S(2)}) async-start(), calls=%async_computation.14 | async-start | bytes 9437184 | tf_op jit(solution)/shard_map/all_gather | solution.py:161
  289.4 4.4 collective-permute-start
  289.5 10.6 copy-start.3
  298.6 92.9 %collective-permute-start.1 = (bf16[512,4096]{1,0:T(8,128)(2,1)}, bf16[512,4096]{1,0:T(8,128)(2,1)}, u32[]{:S(2)}, u32[]{:S(2)}) collective-permute-start(bf16[512,4096]{1,0:T(8,128)(2,1)} %maximum_select_fusion.2), channel_id=1, source_target_pairs={{0,8},{4,12},{8,0},{12,4},{16,24},{20,28},{24,16},{28,20},{1,9},{5... | collective-permute-start | bytes 12582920 | tf_op jit(solution)/shard_map/ppermute | solution.py:27
  301.2 466.9 %reduce-scatter.16.cloned.1.call-start = ((), (), s32[]{:S(2)}) async-start(), calls=%async_computation.17 | async-start | bytes 5242880 | tf_op jit(solution)/shard_map/reduce_scatter | solution.py:199
  402.5 215.7 %collective-permute-start.2 = (bf16[1024,4096]{1,0:T(8,128)(2,1)}, bf16[1024,4096]{1,0:T(8,128)(2,1)}, u32[]{:S(2)}, u32[]{:S(2)}) collective-permute-start(bf16[1024,4096]{1,0:T(8,128)(2,1)} %maximum_select_fusion.1), channel_id=1, source_target_pairs={{0,16},{4,20},{8,24},{12,28},{16,0},{20,4},{24,8},{28,12},{1,17},{... | collective-permute-start | bytes 25165832 | tf_op jit(solution)/shard_map/ppermute | solution.py:27
  690.7 77.4 %copy-start.1 = (bf16[2,128,2048]{2,1,0:T(8,128)(2,1)S(1)}, bf16[2,128,2048]{2,1,0:T(8,128)(2,1)}, u32[]{:S(2)}) copy-start(bf16[2,128,2048]{2,1,0:T(8,128)(2,1)} %reduce-scatter.12.cloned.1.call-done) | copy-start | bytes 3145732
  690.7 79.5 %copy-start.2 = (bf16[2,128,2048]{2,1,0:T(8,128)(2,1)S(1)}, bf16[2,128,2048]{2,1,0:T(8,128)(2,1)}, u32[]{:S(2)}) copy-start(bf16[2,128,2048]{2,1,0:T(8,128)(2,1)} %param.23) | copy-start | bytes 3145732
  690.7 164.1 %all-gather.21.cloned.1.call-start = ((), (), s32[]{:S(2)}) async-start(), calls=%async_computation.18 | async-start | bytes 5242880 | tf_op jit(solution)/shard_map/all_gather | solution.py:241
  773.4 255.5 %reduce-scatter.18.cloned.1.call-start = ((), (), s32[]{:S(2)}) async-start(), calls=%async_computation.19 | async-start | bytes 5242880 | tf_op jit(solution)/shard_map/reduce_scatter | solution.py:199
  869.9 9.6 copy-start.20
  869.9 9.6 copy-start.22
  929.2 10.4 copy-start.5
  929.2 10.4 copy-start.7
  929.2 10.4 copy-start.12
  939.5 1.6 copy-start.16
  941.2 7.2 copy-start.8
  948.4 5.1 copy-start.13
  953.4 150.7 %reduce-scatter.26.cloned.1.call-start = ((), (), s32[]{:S(2)}) async-start(), calls=%async_computation.23 | async-start | bytes 9437184 | tf_op jit(solution)/shard_map/reduce_scatter | solution.py:230
  967.8 180.7 %reduce-scatter.22.cloned.1.call-start = ((), (), s32[]{:S(2)}) async-start(), calls=%async_computation.21 | async-start | bytes 2359296 | tf_op jit(solution)/shard_map/reduce_scatter | solution.py:273
  974.1 223.8 %reduce-scatter.20.cloned.1.call-start = ((), (), s32[]{:S(2)}) async-start(), calls=%async_computation.20 | async-start | bytes 3538944 | tf_op jit(solution)/shard_map/reduce_scatter | solution.py:270
  982.1 294.8 %reduce-scatter.14.cloned.1.call-start = ((), (), s32[]{:S(2)}) async-start(), calls=%async_computation.15 | async-start | bytes 5242880 | tf_op jit(solution)/shard_map/reduce_scatter | solution.py:199
  996.3 32.6 %copy-start.24 = (f32[1,2048]{1,0:T(1,128)S(1)}, f32[1,2048]{1,0:T(1,128)}, u32[]{:S(2)}) copy-start(f32[1,2048]{1,0:T(1,128)} %copy-done.23) | copy-start | bytes 24580
  996.3 32.6 %copy-start.27 = (f32[2,128]{1,0:T(2,128)S(1)}, f32[2,128]{1,0:T(2,128)}, u32[]{:S(2)}) copy-start(f32[2,128]{1,0:T(2,128)} %copy-done.26) | copy-start | bytes 3076
  996.3 420.9 %reduce-scatter.28.cloned.1.call-start = ((), (), s32[]{:S(2)}) async-start(), calls=%async_computation.24 | async-start | bytes 1081344
  1032.2 501.3 %reduce-scatter.24.cloned.1.call-start = ((), (), s32[]{:S(2)}) async-start(), calls=%async_computation.22 | async-start | bytes 18874368 | tf_op jit(solution)/shard_map/reduce_scatter | solution.py:234
  1148.5 9.0 copy-start.15
  1201.5 216.8 %copy-start.30 = (f32[64]{0:T(128)S(1)}, f32[64]{0:T(128)}, u32[]{:S(2)}) copy-start(f32[64]{0:T(128)} %param.27) | copy-start | bytes 772
  1201.5 216.8 %copy-start.32 = (f32[64]{0:T(128)S(1)}, f32[64]{0:T(128)}, u32[]{:S(2)}) copy-start(f32[64]{0:T(128)} %param.33) | copy-start | bytes 772
  1201.5 216.8 %copy-start.33 = (f32[64]{0:T(128)S(1)}, f32[64]{0:T(128)}, u32[]{:S(2)}) copy-start(f32[64]{0:T(128)} %param.39) | copy-start | bytes 772
  1201.5 217.3 %copy-start.31 = (f32[64]{0:T(128)S(1)}, f32[64]{0:T(128)}, u32[]{:S(2)}) copy-start(f32[64]{0:T(128)} %param.24) | copy-start | bytes 772
  1201.5 217.3 %copy-start.34 = (f32[64]{0:T(128)S(1)}, f32[64]{0:T(128)}, u32[]{:S(2)}) copy-start(f32[64]{0:T(128)} %param.30) | copy-start | bytes 772
  1201.5 217.3 %copy-start.35 = (f32[64]{0:T(128)S(1)}, f32[64]{0:T(128)}, u32[]{:S(2)}) copy-start(f32[64]{0:T(128)} %param.36) | copy-start | bytes 772
  1418.2 140.8 %copy-start.28 = (f32[64,1]{0,1:T(1,128)}, f32[64,1]{0,1:T(1,128)S(1)}, u32[]{:S(2)}) copy-start(f32[64,1]{0,1:T(1,128)S(1)} %copy.120) | copy-start | bytes 772
  1418.3 140.7 %copy-start.29 = (f32[64,1]{0,1:T(1,128)}, f32[64,1]{0,1:T(1,128)S(1)}, u32[]{:S(2)}) copy-start(f32[64,1]{0,1:T(1,128)S(1)} %copy.119) | copy-start | bytes 772
Sparse Core Ops, SparseCore 0:
  10.5 34.9 all-gather.10
  84.1 76.9 all-gather.8
  163.6 26.5 all-gather.12
  204.4 74.9 reduce-scatter.11
  283.8 81.2 all-gather.14
  366.5 79.2 all-gather.18
  448.2 88.2 all-gather.16
  690.8 77.2 reduce-scatter.15
  773.5 81.2 all-gather.20
  953.6 75.2 reduce-scatter.17
  1032.4 71.7 reduce-scatter.25
  1107.3 41.0 reduce-scatter.21
  1151.8 46.0 reduce-scatter.19
  1200.1 76.7 reduce-scatter.13
  1279.6 137.5 reduce-scatter.27
  1420.6 112.8 reduce-scatter.23
